TPU v7x, 32 devices: a whole 2x2x4 slice. The times are simulated.
32 devices in a mesh: mem: 16 (over z, x, core), space: 2 (over y).
Axes of the slice: x: 2, y: 2, z: 4, core: 2. Of those that a mesh axis runs over, the one named last changes fastest.
Arguments:
- prior_sample_set: float32 [512, 64, 128], P('mem', 'space'), may hold values from -6 to 6
- perturbed_obs: float32 [512, 64, 128], P('mem', 'space'), may hold values from -6 to 6
- measured_slot_table: int32 [64, 128], P('space'), may hold values from 0 to 127
- obs_var: float32 [64, 128], P('space'), may hold values from 0.25 to 2
- neighbours: int32 [64, 2], P('space'), may hold values from 0 to 63, as said below
- norm_gain: float32 [64], replicated, may hold values from 0.5 to 1.5
- w_in: bfloat16 [64, 512], replicated, may hold values from -0.75 to 0.75
- b_in: float32 [512], replicated, may hold values from -3 to 3
- w_out: bfloat16 [512, 64], replicated, may hold values from -0.25 to 0.25
- b_out: float32 [64], replicated, may hold values from -1.2 to 1.2
Outputs:
- analysis: float32 [512, 64, 128], P('mem', 'space')
Inputs may be any that keep to these rules, and one draw needn't show every extreme that they name: `neighbours`: row p names 2 different blocks among p - 1, p, p + 1 taken modulo 64, in the order of these offsets. `measured_slot_table`: entry [b, j] names a variable of patch b.
All inputs are finite; a program needn't handle non-finite values.
Results may differ from a plain program's by a relative error of at most 0.0026.
Values sent between devices are 32-bit elements; how exact they have to be, the bound alone decides.
A program may use at most 64 MiB of HBM per device.

v0:
```python
import functools
import jax
import jax.numpy as jnp
from jax import lax
from jax.experimental import pallas as pl
from jax.experimental.pallas import tpu as pltpu
from jax.sharding import PartitionSpec as P

LEV = 64
HOPS = 2
F32 = jnp.float32
BF16 = jnp.bfloat16
MESH = pl.DeviceIdType.MESH


def dot1(a, b):
    return jnp.dot(a, b, preferred_element_type=F32)


def split(a):
    hi = a.astype(BF16)
    return hi, (a - hi.astype(F32)).astype(BF16)


def dot3(a, b):
    ah, al = split(a)
    bh, bl = split(b)
    return dot1(ah, bh) + dot1(ah, bl) + dot1(al, bh)


def doth(a, b):
    return jnp.dot(a, b, preferred_element_type=F32, precision=lax.Precision.HIGHEST)


def sweep_panel(p, rows, lanes):
    cols = [jnp.broadcast_to(p[:, j:j + 1], p.shape) for j in range(8)]
    for j in range(8):
        col = cols[j]
        row = jnp.broadcast_to(p[j:j + 1, :], p.shape)
        inv = 1.0 / jnp.broadcast_to(col[j:j + 1, :], p.shape)
        for i in range(j + 1, 8):
            r = jnp.broadcast_to(cols[i][j:j + 1, :], p.shape) * inv
            cols[i] = jnp.where(rows == j, r, cols[i] - col * r)
        here = lanes == j
        row = jnp.where(here, inv, row * inv)
        p = jnp.where(rows == j, row, jnp.where(here, 0.0, p) - col * row)
    return jnp.where(lanes < 8, -p, p)


def negative_inverse(mats):
    size = mats[0].shape[0]
    rows = lax.broadcasted_iota(jnp.int32, (8, size), 0)
    lanes = lax.broadcasted_iota(jnp.int32, (8, size), 1)

    def step(_, carry):
        new = []
        for a in carry:
            panel = sweep_panel(a[:8], rows, lanes)
            rest = a[8:]
            acc = jnp.where(lax.broadcasted_iota(jnp.int32, rest.shape, 1) < 8, 0.0, rest)
            for j in range(8):
                acc = acc - rest[:, j:j + 1] * panel[j:j + 1, :]
            a = jnp.concatenate([acc, panel], axis=0)
            new.append(pltpu.roll(a, size - 8, 1))
        return tuple(new)

    return lax.fori_loop(0, size // 8, step, tuple(mats), unroll=2)


def kernel(n, ns, prior, pert, slot, var, nbr, gain, w_in, b_in, w_out, b_out, out,
           xb, pb, yb, ib, res, w1, w2,
           xs, xr, ps, pr, ys, yr, isd, ir, os_, orr, loc):
    me = lax.axis_index("mem")
    sp = lax.axis_index("space")
    count = xb.shape[0]
    size = xb.shape[1]
    width = xb.shape[2]
    each = size // n
    gs = 4 if n % 4 == 0 else 1
    groups = n // gs
    grows = gs * each
    hid = w_in.shape[1]
    span = n * count
    total = span * ns
    my_group = me // gs

    def window(m):
        if gs == 1:
            return m
        z = m // 4
        return z * 4 + lax.rem(lax.rem(m // 2, 2) + z, 2) * 2 + lax.rem(m, 2)

    win = window(me)
    first = win * count
    right = (window(lax.rem(win + 1, n)), lax.rem(sp + (win + 1) // n, ns))
    left = (window(lax.rem(win + n - 1, n)), lax.rem(sp + ns - (n - win) // n, ns))

    def partner(i):
        g = lax.rem(my_group + groups - i // gs, groups)
        return g * gs + lax.rem(me + lax.rem(i, gs), gs)

    bar = pltpu.get_barrier_semaphore()

    @pl.loop(1, n)
    def _(k):
        pl.semaphore_signal(bar, inc=1, device_id=(lax.rem(me + k, n), sp), device_id_type=MESH)

    pl.semaphore_signal(bar, inc=1, device_id=left, device_id_type=MESH)
    pl.semaphore_signal(bar, inc=1, device_id=right, device_id_type=MESH)
    pl.semaphore_wait(bar, n + 1)

    def mine(i):
        return pl.ds(pl.multiple_of(i * each, each), each)

    def fwd(src, dst, ss, rs, d):
        return pltpu.make_async_remote_copy(
            src_ref=src.at[pl.ds(window(d) * count, count)], dst_ref=dst.at[:, mine(me), :],
            send_sem=ss.at[d], recv_sem=rs.at[me], device_id=(d, sp), device_id_type=MESH)

    def arrived(src, dst, ss, rs, s):
        return pltpu.make_async_remote_copy(
            src_ref=src.at[pl.ds(window(s) * count, count)], dst_ref=dst.at[:, mine(s), :],
            send_sem=ss.at[s], recv_sem=rs.at[s], device_id=(s, sp), device_id_type=MESH)

    def own(src, dst, i):
        return pltpu.make_async_copy(src.at[pl.ds(first, count)], dst.at[:, mine(me), :], loc.at[i])

    @pl.loop(1, n)
    def _(k):
        fwd(prior, xb, xs, xr, partner(k)).start()

    own(prior, xb, 0).start()
    own(pert, pb, 1).start()

    zero = jnp.zeros((LEV, hid), BF16)
    half = (w_in[...].astype(F32) * 0.5).astype(BF16)
    w1[:LEV, :hid] = half
    w1[:LEV, hid:] = zero
    w1[LEV:, :hid] = zero
    w1[LEV:, hid:] = half
    w2[:LEV, :hid] = w_out[...]
    w2[:LEV, hid:] = zero
    w2[LEV:, :hid] = zero
    w2[LEV:, hid:] = w_out[...]
    gain2 = jnp.concatenate([gain[...], gain[...]], axis=1)
    bi = b_in[...] * 0.5
    bi2 = jnp.concatenate([bi, bi], axis=1)
    bo2 = jnp.concatenate([b_out[...], b_out[...]], axis=1)
    ri = lax.broadcasted_iota(jnp.int32, (width, width), 0)
    ci = lax.broadcasted_iota(jnp.int32, (width, width), 1)
    ones = jnp.where((ri < LEV) == (ci < LEV), 1.0 / LEV, 0.0).astype(BF16)
    hots = [jnp.where(slot[pl.ds(first + c, 1), :] == ri, 1.0, 0.0).astype(BF16) for c in range(count)]
    roots = [lax.rsqrt(var[pl.ds(first + c, 1), :]) for c in range(count)]

    own(prior, xb, 0).wait()

    def halo(buf, rows, ss, rs, g, side):
        if side == 0:
            return pltpu.make_async_remote_copy(
                src_ref=buf.at[count, rows, :], dst_ref=buf.at[0, rows, :],
                send_sem=ss.at[0, g], recv_sem=rs.at[0, g], device_id=right, device_id_type=MESH)
        return pltpu.make_async_remote_copy(
            src_ref=buf.at[1, rows, :], dst_ref=buf.at[count + 1, rows, :],
            send_sem=ss.at[1, g], recv_sem=rs.at[1, g], device_id=left, device_id_type=MESH)

    def group_rows(g):
        return pl.ds(pl.multiple_of(g * grows, grows), grows)

    @pl.loop(0, groups)
    def _(t):
        g = lax.rem(my_group + t, groups)
        for q in range(gs):
            s = g * gs + q

            @pl.when(s != me)
            def _():
                arrived(prior, xb, xs, xr, s).wait_recv()

        rows = group_rows(g)
        x = xb[:, rows, :].reshape(count * grows, width)
        for _ in range(HOPS):
            hi, lo = split(x * x)
            inv = lax.rsqrt(dot1(hi, ones) + dot1(lo, ones) + 1e-6)
            normed = (x * inv * gain2).astype(BF16)
            h = dot1(normed, w1[...]) + bi2
            hidden = (h + h * jnp.tanh(h)).astype(BF16)
            x = x + lax.dot_general(hidden, w2[...], (((1,), (1,)), ((), ())), preferred_element_type=F32) + bo2
        x = x.reshape(count, grows, width)
        xb[:, rows, :] = x
        for c in range(count):
            hi, lo = split(x[c])
            yb[c + 1, rows, :] = (dot1(hi, hots[c]) + dot1(lo, hots[c])) * roots[c]
        halo(yb, rows, ys, yr, g, 0).start()
        halo(yb, rows, ys, yr, g, 1).start()

    @pl.loop(0, groups)
    def _(g):
        for side in range(2):
            halo(yb, group_rows(g), ys, yr, g, side).wait_recv()

    @pl.loop(1, n)
    def _(k):
        fwd(pert, pb, ps, pr, partner(k)).start()

    def pick(buf, c, rows, length):
        row = first + c
        patch = sp * span + row
        pair = nbr[pl.ds(row, 1), :]
        a = jnp.broadcast_to(pair[:, 0:1], (length, width)) == lax.rem(patch + total - 1, total)
        b = jnp.broadcast_to(pair[:, 1:2], (length, width)) == lax.rem(patch + 1, total)
        mid = buf[c + 1, rows, :]
        return jnp.concatenate(
            [jnp.where(a, buf[c, rows, :], mid), jnp.where(b, buf[c + 2, rows, :], mid)], axis=1)

    every = pl.ds(0, size)
    grams = []
    for c in range(count):
        y = pick(yb, c, every, size)
        bb = y - jnp.mean(y, axis=0, keepdims=True)
        x = xb[c]
        z = jnp.concatenate([bb, x - jnp.mean(x, axis=0, keepdims=True)], axis=1)
        grams.append(dot3(bb.T, z) * (1.0 / (size - 1)))
    eye = jnp.where(ri == ci, 1.0, 0.0)
    w = width
    pinv = negative_inverse([m[:w, :w] + eye for m in grams])

    own(pert, pb, 1).wait()

    @pl.loop(0, groups)
    def _(t):
        g = lax.rem(my_group + t, groups)
        for q in range(gs):
            s = g * gs + q

            @pl.when(s != me)
            def _():
                arrived(pert, pb, ps, pr, s).wait_recv()

        rows = group_rows(g)
        for c in range(count):
            ib[c + 1, rows, :] = pb[c, rows, :] * roots[c] - yb[c + 1, rows, :]
        halo(ib, rows, isd, ir, g, 0).start()
        halo(ib, rows, isd, ir, g, 1).start()

    es = [doth(pinv[c], grams[c][:w, w:2 * w]) for c in range(count)]
    ts = [grams[c][w:, w:2 * w] + eye + doth(grams[c][w:, :w], es[c]) for c in range(count)]
    fs = [doth(pinv[c], grams[c][:w, 2 * w:]) for c in range(count)]
    tinv = negative_inverse(ts)
    gains = []
    for c in range(count):
        k2 = -doth(tinv[c], grams[c][w:, 2 * w:] + doth(grams[c][w:, :w], fs[c]))
        k1 = doth(es[c], k2) - fs[c]
        gains.append(jnp.concatenate([k1, k2], axis=0))


    def back(d):
        return pltpu.make_async_remote_copy(
            src_ref=res.at[:, mine(d), :], dst_ref=out.at[pl.ds(first, count)],
            send_sem=os_.at[d], recv_sem=orr.at[me], device_id=(d, sp), device_id_type=MESH)

    def returned(s):
        return pltpu.make_async_remote_copy(
            src_ref=res.at[:, mine(s), :], dst_ref=out.at[pl.ds(window(s) * count, count)],
            send_sem=os_.at[s], recv_sem=orr.at[s], device_id=(s, sp), device_id_type=MESH)

    gh = [split(m) for m in gains]

    @pl.loop(0, groups)
    def _(t):
        g = lax.rem(my_group + groups // 2 + t, groups)
        rows = group_rows(g)
        for side in range(2):
            halo(ib, rows, isd, ir, g, side).wait_recv()
        for c in range(count):
            ih, il = split(pick(ib, c, rows, grows))
            res[c, rows, :] = xb[c, rows, :] + dot1(ih, gh[c][0]) + dot1(ih, gh[c][1]) + dot1(il, gh[c][0])
        for q in range(gs):
            d = g * gs + lax.rem(me + q, gs)

            @pl.when(d != me)
            def _():
                back(d).start()

    last = pltpu.make_async_copy(res.at[:, mine(me), :], out.at[pl.ds(first, count)], loc.at[2])
    last.start()

    @pl.loop(0, groups)
    def _(g):
        for side in range(2):
            halo(yb, group_rows(g), ys, yr, g, side).wait_send()
            halo(ib, group_rows(g), isd, ir, g, side).wait_send()

    last.wait()

    @pl.loop(1, n)
    def _(k):
        d = lax.rem(me + k, n)
        fwd(prior, xb, xs, xr, d).wait_send()
        fwd(pert, pb, ps, pr, d).wait_send()
        back(d).wait_send()
        returned(d).wait_recv()


def body(prior, pert, slot, var, nbr, gain, w_in, b_in, w_out, b_out):
    n = lax.axis_size("mem")
    ns = lax.axis_size("space")
    each, span, width = prior.shape
    count = span // n
    size = each * n
    hid = w_in.shape[1]
    vm = pl.BlockSpec(memory_space=pltpu.VMEM)
    anyw = pl.BlockSpec(memory_space=pl.ANY)
    groups = n // (4 if n % 4 == 0 else 1)
    dma = pltpu.SemaphoreType.DMA
    out = pl.pallas_call(
        functools.partial(kernel, n, ns),
        out_shape=jax.ShapeDtypeStruct((span, each, width), F32),
        in_specs=[anyw, anyw, vm, vm, vm, vm, vm, vm, vm, vm],
        out_specs=anyw,
        scratch_shapes=[
            pltpu.VMEM((count, size, width), F32),
            pltpu.VMEM((count, size, width), F32),
            pltpu.VMEM((count + 2, size, width), F32),
            pltpu.VMEM((count + 2, size, width), F32),
            pltpu.VMEM((count, size, width), F32),
            pltpu.VMEM((width, 2 * hid), BF16),
            pltpu.VMEM((width, 2 * hid), BF16),
            dma((n,)), dma((n,)), dma((n,)), dma((n,)),
            dma((2, groups)), dma((2, groups)), dma((2, groups)), dma((2, groups)),
            dma((n,)), dma((n,)), dma((3,)),
        ],
        compiler_params=pltpu.CompilerParams(
            collective_id=0, has_side_effects=True, vmem_limit_bytes=48 * 1024 * 1024),
        name="cycle",
    )(jnp.transpose(prior, (1, 0, 2)), jnp.transpose(pert, (1, 0, 2)), slot, var, nbr,
      gain[None], w_in, b_in[None], w_out.T, b_out[None])
    return jnp.transpose(out, (1, 0, 2))


def solution(mesh):
    in_specs = (
        P("mem", "space", None), P("mem", "space", None),
        P("space", None), P("space", None), P("space", None),
        P(), P(), P(), P(), P(),
    )
    return jax.shard_map(body, mesh=mesh, in_specs=in_specs, out_specs=P("mem", "space", None), check_vma=False)
```

profile of v0, /device:TPU:9, one launch (start us, length us, event | category | flops | bytes accessed | tf_op | source)
XLA Modules:
  0.0 65.3 jit_solution(13704631091341214477)
XLA Ops:
  0.0 0.0 copy-start.7
  0.0 0.7 %copy-done.7 = s32[32,2]{0,1:T(2,128)S(1)} copy-done((s32[32,2]{0,1:T(2,128)S(1)}, s32[32,2]{0,1:T(2,128)}, u32[]{:S(2)}) %copy-start.7) | copy-done | bytes 280
  0.7 0.1 copy.13.nbr
  0.8 0.0 copy-start
  0.8 0.0 copy-start.1
  0.8 0.0 copy-start.2
  0.8 0.0 copy-start.3
  0.8 1.8 %copy_bitcast_fusion = (f32[32,32,128]{2,1,0:T(8,128)S(1)}, f32[32,32,128]{2,1,0:T(8,128)S(1)}) fusion(f32[32,32,128]{2,1,0:T(8,128)} %param.11, f32[32,32,128]{2,1,0:T(8,128)} %param.10), kind=kLoop, calls=%fused_computation | loop fusion | bytes 2097152 | tf_op jit(solution)/shard_map/transpose | solution.py:335
  2.6 0.0 copy-start.4
  2.6 0.0 copy-start.5
  2.7 0.0 copy-start.6
  2.7 0.0 copy-done
  2.7 0.0 copy-done.1
  2.7 0.0 copy-done.2
  2.7 0.0 copy-done.3
  2.7 0.6 copy-done.4
  3.3 0.0 copy-done.5
  3.3 0.0 copy-done.6
  3.3 60.9 %cycle.1 = f32[32,32,128]{2,1,0:T(8,128)S(1)} custom-call(f32[32,32,128]{2,1,0:T(8,128)S(1)} %get-tuple-element.6.prior, f32[32,32,128]{2,1,0:T(8,128)S(1)} %get-tuple-element.5.pert, s32[32,128]{1,0:T(8,128)S(1)} %copy-done.2, f32[32,128]{1,0:T(8,128)S(1)} %copy-done.3, s32[32,2]{1,0:T(8,128)S(1)} %copy.13.nbr, f32[1,64]{1,0:T(1,128)S(1)} %bitcast.12, ...), custom_call_target="tpu_custom_call" | custom-call | tf_op jit(solution)/shard_map/cycle/pallas_call | solution.py:315
  64.2 1.1 %copy.14 = f32[32,32,128]{2,1,0:T(8,128)} copy(f32[32,32,128]{2,0,1:T(8,128)S(1)} %bitcast.9) | data formatting | bytes 1048576 | tf_op jit(solution)/shard_map/transpose | solution.py:337
Async XLA Ops:
  0.0 0.7 %copy-start.7 = (s32[32,2]{0,1:T(2,128)S(1)}, s32[32,2]{0,1:T(2,128)}, u32[]{:S(2)}) copy-start(s32[32,2]{0,1:T(2,128)} %param.14) | copy-start | bytes 772
  0.8 1.9 %copy-start = (bf16[64,512]{1,0:T(8,128)(2,1)S(1)}, bf16[64,512]{1,0:T(8,128)(2,1)}, u32[]{:S(2)}) copy-start(bf16[64,512]{1,0:T(8,128)(2,1)} %w_in.1) | copy-start | bytes 196612
  0.8 1.9 %copy-start.1 = (bf16[512,64]{0,1:T(8,128)(2,1)S(1)}, bf16[512,64]{0,1:T(8,128)(2,1)}, u32[]{:S(2)}) copy-start(bf16[512,64]{0,1:T(8,128)(2,1)} %param.18) | copy-start | bytes 196612
  0.8 1.9 %copy-start.2 = (s32[32,128]{1,0:T(8,128)S(1)}, s32[32,128]{1,0:T(8,128)}, u32[]{:S(2)}) copy-start(s32[32,128]{1,0:T(8,128)} %slot.1) | copy-start | bytes 49156
  0.8 1.9 %copy-start.3 = (f32[32,128]{1,0:T(8,128)S(1)}, f32[32,128]{1,0:T(8,128)}, u32[]{:S(2)}) copy-start(f32[32,128]{1,0:T(8,128)} %var.1) | copy-start | bytes 49156
  2.6 0.7 %copy-start.4 = (f32[512]{0:T(512)S(1)}, f32[512]{0:T(512)}, u32[]{:S(2)}) copy-start(f32[512]{0:T(512)} %param.17) | copy-start | bytes 6148
  2.6 0.7 %copy-start.5 = (f32[64]{0:T(128)S(1)}, f32[64]{0:T(128)}, u32[]{:S(2)}) copy-start(f32[64]{0:T(128)} %param.15) | copy-start | bytes 772
  2.7 0.7 %copy-start.6 = (f32[64]{0:T(128)S(1)}, f32[64]{0:T(128)}, u32[]{:S(2)}) copy-start(f32[64]{0:T(128)} %param.19) | copy-start | bytes 772
where the time goes:
time: 65.5 us; the launch traced here: 65.3 us
  Pallas kernels  60.9 us (93%)
  local copies, waits for them, and re-layouts  4.36 us (7%)
    pallas_call x1, Pallas kernels, body(): pl.pallas_call(functools.partial(kernel, n, ns), out_shape=jax.ShapeDtype...  60.9 us
    transpose x1, local copies, waits for them, and re-layouts, body(): jnp.transpose(pert, (1, 0, 2))  1.85 us
    unnamed x17, local copies, waits for them, and re-layouts  1.41 us

commit v1 on v0

--- a/solution.py
+++ b/solution.py
@@ -32,39 +32,67 @@
     return jnp.dot(a, b, preferred_element_type=F32, precision=lax.Precision.HIGHEST)
 
 
-def sweep_panel(p, rows, lanes):
-    cols = [jnp.broadcast_to(p[:, j:j + 1], p.shape) for j in range(8)]
-    for j in range(8):
-        col = cols[j]
-        row = jnp.broadcast_to(p[j:j + 1, :], p.shape)
-        inv = 1.0 / jnp.broadcast_to(col[j:j + 1, :], p.shape)
-        for i in range(j + 1, 8):
-            r = jnp.broadcast_to(cols[i][j:j + 1, :], p.shape) * inv
-            cols[i] = jnp.where(rows == j, r, cols[i] - col * r)
-        here = lanes == j
-        row = jnp.where(here, inv, row * inv)
-        p = jnp.where(rows == j, row, jnp.where(here, 0.0, p) - col * row)
-    return jnp.where(lanes < 8, -p, p)
-
-
-def negative_inverse(mats):
+def spread_row(v, r):
+    return jnp.broadcast_to(v[r:r + 1, :], v.shape)
+
+def sweep(p, base, rows, lanes):
+    cols = [jnp.broadcast_to(p[:, base + j:base + j + 1], p.shape) for j in range(8)]
+    for j in range(0, 8, 2):
+        ca, cb = cols[j], cols[j + 1]
+        al, be, de = spread_row(ca, j), spread_row(cb, j), spread_row(cb, j + 1)
+        inv = 1.0 / (al * de - be * be)
+        ra, rb = rows == j, rows == j + 1
+        na = jnp.where(ra, -1.0, jnp.where(rb, 0.0, ca))
+        nb = jnp.where(rb, -1.0, jnp.where(ra, 0.0, cb))
+
+        def step(v, a, b):
+            t = na * (de * a - be * b) + nb * (al * b - be * a)
+            return jnp.where(ra | rb, 0.0, v) - t * inv
+
+        for i in range(j + 2, 8):
+            cols[i] = step(cols[i], spread_row(cols[i], j), spread_row(cols[i], j + 1))
+        la, lb = lanes == base + j, lanes == base + j + 1
+        a = jnp.where(la, 1.0, jnp.where(lb, 0.0, spread_row(p, j)))
+        b = jnp.where(lb, 1.0, jnp.where(la, 0.0, spread_row(p, j + 1)))
+        p = step(jnp.where(la | lb, 0.0, p), a, b)
+    return p
+
+def inverses(mats, nb=16):
     size = mats[0].shape[0]
     rows = lax.broadcasted_iota(jnp.int32, (8, size), 0)
     lanes = lax.broadcasted_iota(jnp.int32, (8, size), 1)
-
-    def step(_, carry):
-        new = []
-        for a in carry:
-            panel = sweep_panel(a[:8], rows, lanes)
-            rest = a[8:]
-            acc = jnp.where(lax.broadcasted_iota(jnp.int32, rest.shape, 1) < 8, 0.0, rest)
-            for j in range(8):
-                acc = acc - rest[:, j:j + 1] * panel[j:j + 1, :]
-            a = jnp.concatenate([acc, panel], axis=0)
-            new.append(pltpu.roll(a, size - 8, 1))
-        return tuple(new)
-
-    return lax.fori_loop(0, size // 8, step, tuple(mats), unroll=2)
+    wide = lax.broadcasted_iota(jnp.int32, (size, size), 1)
+    mats = list(mats)
+    for lo in range(0, size, nb):
+        panels = [[a[lo + q:lo + q + 8] for q in range(0, nb, 8)] for a in mats]
+        for q in range(nb // 8):
+            base = lo + 8 * q
+            here = (lanes >= base) & (lanes < base + 8)
+            for m in panels:
+                m[q] = sweep(m[q], base, rows, lanes)
+            for m in panels:
+                for i in range(nb // 8):
+                    if i != q:
+                        acc = jnp.where(here, 0.0, m[i])
+                        for j in range(8):
+                            acc = acc - m[i][:, base + j:base + j + 1] * m[q][j:j + 1, :]
+                        m[i] = acc
+        hole = (wide >= lo) & (wide < lo + nb)
+        for k, a in enumerate(mats):
+            p = jnp.concatenate(panels[k], axis=0)
+            parts = [p]
+            if lo: parts.insert(0, jnp.zeros((lo, size), F32))
+            if lo + nb < size: parts.append(jnp.zeros((size - lo - nb, size), F32))
+            pad = jnp.concatenate(parts, axis=0)
+            out = [p]
+            if lo:
+                t = a[:lo]
+                out.insert(0, jnp.where(hole[:lo], 0.0, t) - doth(t, pad))
+            if lo + nb < size:
+                t = a[lo + nb:]
+                out.append(jnp.where(hole[lo + nb:], 0.0, t) - doth(t, pad))
+            mats[k] = jnp.concatenate(out, axis=0)
+    return mats
 
 
 def kernel(n, ns, prior, pert, slot, var, nbr, gain, w_in, b_in, w_out, b_out, out,
@@ -84,16 +112,26 @@
     total = span * ns
     my_group = me // gs
 
-    def window(m):
+    def window(m, p):
+        w = m
+        if gs == 4:
+            z = m // 4
+            w = z * 4 + lax.rem(lax.rem(m // 2, 2) + z, 2) * 2 + lax.rem(m, 2)
+        return jnp.where(lax.rem(p, 2) == 0, w, n - 1 - w)
+
+    def holder(w, p):
+        w = jnp.where(lax.rem(p, 2) == 0, w, n - 1 - w)
         if gs == 1:
-            return m
-        z = m // 4
-        return z * 4 + lax.rem(lax.rem(m // 2, 2) + z, 2) * 2 + lax.rem(m, 2)
-
-    win = window(me)
+            return w
+        z = w // 4
+        return z * 4 + lax.rem(lax.rem(w // 2, 2) + z, 2) * 2 + lax.rem(w, 2)
+
+    win = window(me, sp)
     first = win * count
-    right = (window(lax.rem(win + 1, n)), lax.rem(sp + (win + 1) // n, ns))
-    left = (window(lax.rem(win + n - 1, n)), lax.rem(sp + ns - (n - win) // n, ns))
+    rsp = lax.rem(sp + (win + 1) // n, ns)
+    lsp = lax.rem(sp + ns - (n - win) // n, ns)
+    right = (holder(lax.rem(win + 1, n), rsp), rsp)
+    left = (holder(lax.rem(win + n - 1, n), lsp), lsp)
 
     def partner(i):
         g = lax.rem(my_group + groups - i // gs, groups)
@@ -114,12 +152,12 @@
 
     def fwd(src, dst, ss, rs, d):
         return pltpu.make_async_remote_copy(
-            src_ref=src.at[pl.ds(window(d) * count, count)], dst_ref=dst.at[:, mine(me), :],
+            src_ref=src.at[pl.ds(window(d, sp) * count, count)], dst_ref=dst.at[:, mine(me), :],
             send_sem=ss.at[d], recv_sem=rs.at[me], device_id=(d, sp), device_id_type=MESH)
 
     def arrived(src, dst, ss, rs, s):
         return pltpu.make_async_remote_copy(
-            src_ref=src.at[pl.ds(window(s) * count, count)], dst_ref=dst.at[:, mine(s), :],
+            src_ref=src.at[pl.ds(window(s, sp) * count, count)], dst_ref=dst.at[:, mine(s), :],
             send_sem=ss.at[s], recv_sem=rs.at[s], device_id=(s, sp), device_id_type=MESH)
 
     def own(src, dst, i):
@@ -193,14 +231,14 @@
         halo(yb, rows, ys, yr, g, 0).start()
         halo(yb, rows, ys, yr, g, 1).start()
 
+    @pl.loop(1, n)
+    def _(k):
+        fwd(pert, pb, ps, pr, partner(k)).start()
+
     @pl.loop(0, groups)
     def _(g):
         for side in range(2):
             halo(yb, group_rows(g), ys, yr, g, side).wait_recv()
-
-    @pl.loop(1, n)
-    def _(k):
-        fwd(pert, pb, ps, pr, partner(k)).start()
 
     def pick(buf, c, rows, length):
         row = first + c
@@ -222,7 +260,7 @@
         grams.append(dot3(bb.T, z) * (1.0 / (size - 1)))
     eye = jnp.where(ri == ci, 1.0, 0.0)
     w = width
-    pinv = negative_inverse([m[:w, :w] + eye for m in grams])
+    pinv = inverses([m[:w, :w] + eye for m in grams])
 
     own(pert, pb, 1).wait()
 
@@ -243,15 +281,14 @@
         halo(ib, rows, isd, ir, g, 1).start()
 
     es = [doth(pinv[c], grams[c][:w, w:2 * w]) for c in range(count)]
-    ts = [grams[c][w:, w:2 * w] + eye + doth(grams[c][w:, :w], es[c]) for c in range(count)]
+    ts = [grams[c][w:, w:2 * w] + eye - doth(grams[c][w:, :w], es[c]) for c in range(count)]
     fs = [doth(pinv[c], grams[c][:w, 2 * w:]) for c in range(count)]
-    tinv = negative_inverse(ts)
+    tinv = inverses(ts)
     gains = []
     for c in range(count):
-        k2 = -doth(tinv[c], grams[c][w:, 2 * w:] + doth(grams[c][w:, :w], fs[c]))
-        k1 = doth(es[c], k2) - fs[c]
+        k2 = doth(tinv[c], grams[c][w:, 2 * w:] - doth(grams[c][w:, :w], fs[c]))
+        k1 = fs[c] - doth(es[c], k2)
         gains.append(jnp.concatenate([k1, k2], axis=0))
-
 
     def back(d):
         return pltpu.make_async_remote_copy(
@@ -260,7 +297,7 @@
 
     def returned(s):
         return pltpu.make_async_remote_copy(
-            src_ref=res.at[:, mine(s), :], dst_ref=out.at[pl.ds(window(s) * count, count)],
+            src_ref=res.at[:, mine(s), :], dst_ref=out.at[pl.ds(window(s, sp) * count, count)],
             send_sem=os_.at[s], recv_sem=orr.at[s], device_id=(s, sp), device_id_type=MESH)
 
     gh = [split(m) for m in gains]

time: 65.5 us -> 56.7 us (0.87)
  Pallas kernels: 60.9 us -> 52 us
    pallas_call x1, Pallas kernels: 60.9 us -> 52 us  [body(): pl.pallas_call(functools.partial(kernel, n, ns), out_shape=jax.ShapeDtype...]
where the time goes in v1:
time: 56.7 us; the launch traced here: 56.5 us
  Pallas kernels  52 us (92%)
  local copies, waits for them, and re-layouts  4.36 us (8%)
    pallas_call x1, Pallas kernels, body(): pl.pallas_call(functools.partial(kernel, n, ns), out_shape=jax.ShapeDtype...  52 us
    transpose x1, local copies, waits for them, and re-layouts, body(): jnp.transpose(pert, (1, 0, 2))  1.85 us
    unnamed x17, local copies, waits for them, and re-layouts  1.41 us

profile of v1, /device:TPU:9, one launch (start us, length us, event | category | flops | bytes accessed | tf_op | source)
XLA Modules:
  0.0 56.5 jit_solution(2202883607215884991)
XLA Ops:
  0.0 0.0 copy-start.7
  0.0 0.7 %copy-done.7 = s32[32,2]{0,1:T(2,128)S(1)} copy-done((s32[32,2]{0,1:T(2,128)S(1)}, s32[32,2]{0,1:T(2,128)}, u32[]{:S(2)}) %copy-start.7) | copy-done | bytes 280
  0.7 0.1 copy.13.nbr
  0.8 0.0 copy-start
  0.8 0.0 copy-start.1
  0.8 0.0 copy-start.2
  0.8 0.0 copy-start.3
  0.8 1.8 %copy_bitcast_fusion = (f32[32,32,128]{2,1,0:T(8,128)S(1)}, f32[32,32,128]{2,1,0:T(8,128)S(1)}) fusion(f32[32,32,128]{2,1,0:T(8,128)} %param.11, f32[32,32,128]{2,1,0:T(8,128)} %param.10), kind=kLoop, calls=%fused_computation | loop fusion | bytes 2097152 | tf_op jit(solution)/shard_map/transpose | solution.py:372
  2.6 0.0 copy-start.4
  2.6 0.0 copy-start.5
  2.7 0.0 copy-start.6
  2.7 0.0 copy-done
  2.7 0.0 copy-done.1
  2.7 0.0 copy-done.2
  2.7 0.0 copy-done.3
  2.7 0.6 %copy-done.4 = f32[512]{0:T(512)S(1)} copy-done((f32[512]{0:T(512)S(1)}, f32[512]{0:T(512)}, u32[]{:S(2)}) %copy-start.4) | copy-done | bytes 2072
  3.3 0.0 copy-done.5
  3.3 0.0 copy-done.6
  3.3 52.0 %cycle.1 = f32[32,32,128]{2,1,0:T(8,128)S(1)} custom-call(f32[32,32,128]{2,1,0:T(8,128)S(1)} %get-tuple-element.6.prior, f32[32,32,128]{2,1,0:T(8,128)S(1)} %get-tuple-element.5.pert, s32[32,128]{1,0:T(8,128)S(1)} %copy-done.2, f32[32,128]{1,0:T(8,128)S(1)} %copy-done.3, s32[32,2]{1,0:T(8,128)S(1)} %copy.13.nbr, f32[1,64]{1,0:T(1,128)S(1)} %bitcast.12, ...), custom_call_target="tpu_custom_call" | custom-call | tf_op jit(solution)/shard_map/cycle/pallas_call | solution.py:352
  55.4 1.1 %copy.14 = f32[32,32,128]{2,1,0:T(8,128)} copy(f32[32,32,128]{2,0,1:T(8,128)S(1)} %bitcast.9) | data formatting | bytes 1048576 | tf_op jit(solution)/shard_map/transpose | solution.py:374
Async XLA Ops:
  0.0 0.7 %copy-start.7 = (s32[32,2]{0,1:T(2,128)S(1)}, s32[32,2]{0,1:T(2,128)}, u32[]{:S(2)}) copy-start(s32[32,2]{0,1:T(2,128)} %param.14) | copy-start | bytes 772
  0.8 1.9 %copy-start = (bf16[64,512]{1,0:T(8,128)(2,1)S(1)}, bf16[64,512]{1,0:T(8,128)(2,1)}, u32[]{:S(2)}) copy-start(bf16[64,512]{1,0:T(8,128)(2,1)} %w_in.1) | copy-start | bytes 196612
  0.8 1.9 %copy-start.1 = (bf16[512,64]{0,1:T(8,128)(2,1)S(1)}, bf16[512,64]{0,1:T(8,128)(2,1)}, u32[]{:S(2)}) copy-start(bf16[512,64]{0,1:T(8,128)(2,1)} %param.18) | copy-start | bytes 196612
  0.8 1.9 %copy-start.2 = (s32[32,128]{1,0:T(8,128)S(1)}, s32[32,128]{1,0:T(8,128)}, u32[]{:S(2)}) copy-start(s32[32,128]{1,0:T(8,128)} %slot.1) | copy-start | bytes 49156
  0.8 1.9 %copy-start.3 = (f32[32,128]{1,0:T(8,128)S(1)}, f32[32,128]{1,0:T(8,128)}, u32[]{:S(2)}) copy-start(f32[32,128]{1,0:T(8,128)} %var.1) | copy-start | bytes 49156
  2.6 0.7 %copy-start.4 = (f32[512]{0:T(512)S(1)}, f32[512]{0:T(512)}, u32[]{:S(2)}) copy-start(f32[512]{0:T(512)} %param.17) | copy-start | bytes 6148
  2.6 0.7 %copy-start.5 = (f32[64]{0:T(128)S(1)}, f32[64]{0:T(128)}, u32[]{:S(2)}) copy-start(f32[64]{0:T(128)} %param.15) | copy-start | bytes 772
  2.7 0.7 %copy-start.6 = (f32[64]{0:T(128)S(1)}, f32[64]{0:T(128)}, u32[]{:S(2)}) copy-start(f32[64]{0:T(128)} %param.19) | copy-start | bytes 772

commit v2 on v1

--- a/solution.py
+++ b/solution.py
@@ -20,12 +20,6 @@
 def split(a):
     hi = a.astype(BF16)
     return hi, (a - hi.astype(F32)).astype(BF16)
-
-
-def dot3(a, b):
-    ah, al = split(a)
-    bh, bl = split(b)
-    return dot1(ah, bh) + dot1(ah, bl) + dot1(al, bh)
 
 
 def doth(a, b):
@@ -95,9 +89,12 @@
     return mats
 
 
-def kernel(n, ns, prior, pert, slot, var, nbr, gain, w_in, b_in, w_out, b_out, out,
-           xb, pb, yb, ib, res, w1, w2,
-           xs, xr, ps, pr, ys, yr, isd, ir, os_, orr, loc):
+def kernel(n, ns, prior_in, pert_in, *refs):
+    small_in, refs = refs[:8], refs[8:]
+    out, raw, rawp, prior, pert = refs[:5]
+    slot, var, nbr, gain, w_in, b_in, w_out, b_out = small = refs[5:13]
+    (xb, pb, yb, ib, res, w1, w2,
+     xs, xr, ps, pr, ys, yr, isd, ir, os_, orr, loc) = refs[13:]
     me = lax.axis_index("mem")
     sp = lax.axis_index("space")
     count = xb.shape[0]
@@ -137,6 +134,11 @@
         g = lax.rem(my_group + groups - i // gs, groups)
         return g * gs + lax.rem(me + lax.rem(i, gs), gs)
 
+    loads = [pltpu.make_async_copy(prior_in, raw, loc.at[0]), pltpu.make_async_copy(pert_in, rawp, loc.at[1])]
+    loads += [pltpu.make_async_copy(a, b, loc.at[3 + i]) for i, (a, b) in enumerate(zip(small_in, small))]
+    for load in loads:
+        load.start()
+
     bar = pltpu.get_barrier_semaphore()
 
     @pl.loop(1, n)
@@ -145,10 +147,23 @@
 
     pl.semaphore_signal(bar, inc=1, device_id=left, device_id_type=MESH)
     pl.semaphore_signal(bar, inc=1, device_id=right, device_id_type=MESH)
-    pl.semaphore_wait(bar, n + 1)
 
     def mine(i):
         return pl.ds(pl.multiple_of(i * each, each), each)
+
+    def by_patch(src, dst):
+        @pl.loop(0, span)
+        def _(p):
+            for m in range(0, each, 8):
+                dst[p, pl.ds(m, 8), :] = src[pl.ds(p + m * span, 8, stride=span), :]
+
+    def keep(src, dst):
+        for c in range(count):
+            dst[c, mine(me), :] = src[first + c]
+
+    loads[0].wait()
+    by_patch(raw, prior)
+    pl.semaphore_wait(bar, n + 1)
 
     def fwd(src, dst, ss, rs, d):
         return pltpu.make_async_remote_copy(
@@ -160,15 +175,15 @@
             src_ref=src.at[pl.ds(window(s, sp) * count, count)], dst_ref=dst.at[:, mine(s), :],
             send_sem=ss.at[s], recv_sem=rs.at[s], device_id=(s, sp), device_id_type=MESH)
 
-    def own(src, dst, i):
-        return pltpu.make_async_copy(src.at[pl.ds(first, count)], dst.at[:, mine(me), :], loc.at[i])
-
     @pl.loop(1, n)
     def _(k):
         fwd(prior, xb, xs, xr, partner(k)).start()
 
-    own(prior, xb, 0).start()
-    own(pert, pb, 1).start()
+    keep(prior, xb)
+    for load in loads[1:]:
+        load.wait()
+    by_patch(rawp, pert)
+    keep(pert, pb)
 
     zero = jnp.zeros((LEV, hid), BF16)
     half = (w_in[...].astype(F32) * 0.5).astype(BF16)
@@ -189,8 +204,17 @@
     ones = jnp.where((ri < LEV) == (ci < LEV), 1.0 / LEV, 0.0).astype(BF16)
     hots = [jnp.where(slot[pl.ds(first + c, 1), :] == ri, 1.0, 0.0).astype(BF16) for c in range(count)]
     roots = [lax.rsqrt(var[pl.ds(first + c, 1), :]) for c in range(count)]
-
-    own(prior, xb, 0).wait()
+    near = lax.broadcasted_iota(jnp.int32, (2, span), 1)
+
+    def named(c, side, offset):
+        hit = (nbr[...] == lax.rem(sp * span + first + c + offset + total, total)) & (near == first + c)
+        return jnp.max(jnp.where(hit, 1.0, 0.0), axis=1, keepdims=True)[side:side + 1, :]
+
+    on_left = [named(c, 0, -1) for c in range(count)]
+    on_right = [named(c, 1, 1) for c in range(count)]
+
+    def either(flag, a, b):
+        return jnp.where(jnp.broadcast_to(flag, a.shape) > 0.5, a, b)
 
     def halo(buf, rows, ss, rs, g, side):
         if side == 0:
@@ -235,58 +259,85 @@
     def _(k):
         fwd(pert, pb, ps, pr, partner(k)).start()
 
+    w = width
+    eye = jnp.where(ri == ci, 1.0, 0.0)
+
+    def anomaly(v):
+        return split(v - jnp.mean(v, axis=0, keepdims=True))
+
+    def products(i, right_sides):
+        hi, lo = obs[i]
+        hi, lo = hi.T, lo.T
+        rh = jnp.concatenate([r[0] for r in right_sides], axis=1)
+        rl = jnp.concatenate([r[1] for r in right_sides], axis=1)
+        full = (dot1(hi, rh) + dot1(hi, rl) + dot1(lo, rh)) * (1.0 / (size - 1))
+        return [full[:, k * w:(k + 1) * w] for k in range(len(right_sides))]
+
+    obs = {c + 1: anomaly(yb[c + 1]) for c in range(count)}
+    states = [anomaly(xb[c]) for c in range(count)]
+    yy, yx = {}, {}
+
+    def multiply(i, js, cs):
+        if js or cs:
+            parts = products(i, [obs[j] for j in js] + [states[c] for c in cs])
+            for j in js:
+                yy[i, j] = parts.pop(0)
+            for c in cs:
+                yx[i, c] = parts.pop(0)
+
+    last_one = count + 1
+    for i in range(1, count + 1):
+        multiply(i, [j for j in range(i, min(i + 2, count) + 1)], [c for c in range(count) if abs(c + 1 - i) < 2])
+
     @pl.loop(0, groups)
     def _(g):
         for side in range(2):
             halo(yb, group_rows(g), ys, yr, g, side).wait_recv()
 
-    def pick(buf, c, rows, length):
-        row = first + c
-        patch = sp * span + row
-        pair = nbr[pl.ds(row, 1), :]
-        a = jnp.broadcast_to(pair[:, 0:1], (length, width)) == lax.rem(patch + total - 1, total)
-        b = jnp.broadcast_to(pair[:, 1:2], (length, width)) == lax.rem(patch + 1, total)
-        mid = buf[c + 1, rows, :]
-        return jnp.concatenate(
-            [jnp.where(a, buf[c, rows, :], mid), jnp.where(b, buf[c + 2, rows, :], mid)], axis=1)
-
-    every = pl.ds(0, size)
-    grams = []
+    obs[0] = anomaly(yb[0])
+    obs[last_one] = anomaly(yb[last_one])
+    multiply(0, [j for j in range(0, min(2, last_one) + 1)], [0])
+    for i in range(max(1, last_one - 2), last_one):
+        multiply(i, [last_one], [])
+    multiply(last_one, [last_one], [count - 1])
+
+    s11, s12, s22, g1, g2 = [], [], [], [], []
     for c in range(count):
-        y = pick(yb, c, every, size)
-        bb = y - jnp.mean(y, axis=0, keepdims=True)
-        x = xb[c]
-        z = jnp.concatenate([bb, x - jnp.mean(x, axis=0, keepdims=True)], axis=1)
-        grams.append(dot3(bb.T, z) * (1.0 / (size - 1)))
-    eye = jnp.where(ri == ci, 1.0, 0.0)
-    w = width
-    pinv = inverses([m[:w, :w] + eye for m in grams])
-
-    own(pert, pb, 1).wait()
-
-    @pl.loop(0, groups)
-    def _(t):
-        g = lax.rem(my_group + t, groups)
-        for q in range(gs):
-            s = g * gs + q
-
-            @pl.when(s != me)
-            def _():
-                arrived(pert, pb, ps, pr, s).wait_recv()
-
-        rows = group_rows(g)
-        for c in range(count):
-            ib[c + 1, rows, :] = pb[c, rows, :] * roots[c] - yb[c + 1, rows, :]
-        halo(ib, rows, isd, ir, g, 0).start()
-        halo(ib, rows, isd, ir, g, 1).start()
-
-    es = [doth(pinv[c], grams[c][:w, w:2 * w]) for c in range(count)]
-    ts = [grams[c][w:, w:2 * w] + eye - doth(grams[c][w:, :w], es[c]) for c in range(count)]
-    fs = [doth(pinv[c], grams[c][:w, 2 * w:]) for c in range(count)]
+        e = c + 1
+        s11.append(either(on_left[c], yy[e - 1, e - 1], yy[e, e]) + eye)
+        s22.append(either(on_right[c], yy[e + 1, e + 1], yy[e, e]) + eye)
+        s12.append(either(on_left[c], either(on_right[c], yy[e - 1, e + 1], yy[e - 1, e]), yy[e, e + 1]))
+        g1.append(either(on_left[c], yx[e - 1, c], yx[e, c]))
+        g2.append(either(on_right[c], yx[e + 1, c], yx[e, c]))
+    s21 = [m.T for m in s12]
+
+    def innovate(start, stop):
+        @pl.loop(start, stop)
+        def _(t):
+            g = lax.rem(my_group + t, groups)
+            for q in range(gs):
+                s = g * gs + q
+
+                @pl.when(s != me)
+                def _():
+                    arrived(pert, pb, ps, pr, s).wait_recv()
+
+            rows = group_rows(g)
+            for c in range(count):
+                ib[c + 1, rows, :] = pb[c, rows, :] * roots[c] - yb[c + 1, rows, :]
+            halo(ib, rows, isd, ir, g, 0).start()
+            halo(ib, rows, isd, ir, g, 1).start()
+
+    pinv = inverses(s11)
+    innovate(0, 2)
+    es = [doth(pinv[c], s12[c]) for c in range(count)]
+    ts = [s22[c] - doth(s21[c], es[c]) for c in range(count)]
+    fs = [doth(pinv[c], g1[c]) for c in range(count)]
     tinv = inverses(ts)
+    innovate(2, groups)
     gains = []
     for c in range(count):
-        k2 = doth(tinv[c], grams[c][w:, 2 * w:] - doth(grams[c][w:, :w], fs[c]))
+        k2 = doth(tinv[c], g2[c] - doth(s21[c], fs[c]))
         k1 = fs[c] - doth(es[c], k2)
         gains.append(jnp.concatenate([k1, k2], axis=0))
 
@@ -301,6 +352,11 @@
             send_sem=os_.at[s], recv_sem=orr.at[s], device_id=(s, sp), device_id_type=MESH)
 
     gh = [split(m) for m in gains]
+
+    def pick(c, rows):
+        mid = ib[c + 1, rows, :]
+        return jnp.concatenate(
+            [either(on_left[c], ib[c, rows, :], mid), either(on_right[c], ib[c + 2, rows, :], mid)], axis=1)
 
     @pl.loop(0, groups)
     def _(t):
@@ -309,7 +365,7 @@
         for side in range(2):
             halo(ib, rows, isd, ir, g, side).wait_recv()
         for c in range(count):
-            ih, il = split(pick(ib, c, rows, grows))
+            ih, il = split(pick(c, rows))
             res[c, rows, :] = xb[c, rows, :] + dot1(ih, gh[c][0]) + dot1(ih, gh[c][1]) + dot1(il, gh[c][0])
         for q in range(gs):
             d = g * gs + lax.rem(me + q, gs)
@@ -345,16 +401,22 @@
     count = span // n
     size = each * n
     hid = w_in.shape[1]
-    vm = pl.BlockSpec(memory_space=pltpu.VMEM)
     anyw = pl.BlockSpec(memory_space=pl.ANY)
+    hbm = pl.BlockSpec(memory_space=pltpu.HBM)
     groups = n // (4 if n % 4 == 0 else 1)
     dma = pltpu.SemaphoreType.DMA
+    small = [slot, var, nbr.T, gain[None], w_in, b_in[None], w_out.T, b_out[None]]
     out = pl.pallas_call(
         functools.partial(kernel, n, ns),
         out_shape=jax.ShapeDtypeStruct((span, each, width), F32),
-        in_specs=[anyw, anyw, vm, vm, vm, vm, vm, vm, vm, vm],
+        in_specs=[hbm] * (2 + len(small)),
         out_specs=anyw,
         scratch_shapes=[
+            pltpu.VMEM((each * span, width), F32),
+            pltpu.VMEM((each * span, width), F32),
+            pltpu.VMEM((span, each, width), F32),
+            pltpu.VMEM((span, each, width), F32),
+            *[pltpu.VMEM(a.shape, a.dtype) for a in small],
             pltpu.VMEM((count, size, width), F32),
             pltpu.VMEM((count, size, width), F32),
             pltpu.VMEM((count + 2, size, width), F32),
@@ -364,13 +426,12 @@
             pltpu.VMEM((width, 2 * hid), BF16),
             dma((n,)), dma((n,)), dma((n,)), dma((n,)),
             dma((2, groups)), dma((2, groups)), dma((2, groups)), dma((2, groups)),
-            dma((n,)), dma((n,)), dma((3,)),
+            dma((n,)), dma((n,)), dma((3 + len(small),)),
         ],
         compiler_params=pltpu.CompilerParams(
-            collective_id=0, has_side_effects=True, vmem_limit_bytes=48 * 1024 * 1024),
+            collective_id=0, has_side_effects=True, vmem_limit_bytes=67043328),
         name="cycle",
-    )(jnp.transpose(prior, (1, 0, 2)), jnp.transpose(pert, (1, 0, 2)), slot, var, nbr,
-      gain[None], w_in, b_in[None], w_out.T, b_out[None])
+    )(prior.reshape(each * span, width), pert.reshape(each * span, width), *small)
     return jnp.transpose(out, (1, 0, 2))
 
 

time: 56.7 us -> 52.9 us (0.933); the launches traced: 56.5 us -> 51.9 us
  Pallas kernels: 52 us -> 49.7 us
  local copies, waits for them, and re-layouts: 4.36 us -> 2.14 us
    pallas_call x1, Pallas kernels: 52 us -> 49.7 us  [body(): pl.pallas_call(functools.partial(kernel, n, ns), out_shape=jax.ShapeDtype...]
    transpose x1 -> x0, local copies, waits for them, and re-layouts: 1.85 us -> none  [body(): jnp.transpose(pert, (1, 0, 2))]
    unnamed x17 -> x0, local copies, waits for them, and re-layouts: 1.41 us -> none
    transpose x1, local copies, waits for them, and re-layouts: 1.1 us -> 2.14 us  [body(): return jnp.transpose(out, (1, 0, 2))]
where the time goes in v2:
time: 52.9 us; the launch traced here: 51.9 us
  Pallas kernels  49.7 us (94%)
  local copies, waits for them, and re-layouts  2.14 us (4%)
    pallas_call x1, Pallas kernels, body(): pl.pallas_call(functools.partial(kernel, n, ns), out_shape=jax.ShapeDtype...  49.7 us
    transpose x1, local copies, waits for them, and re-layouts, body(): return jnp.transpose(out, (1, 0, 2))  2.14 us

profile of v2, /device:TPU:9, one launch (start us, length us, event | category | flops | bytes accessed | tf_op | source)
XLA Modules:
  0.0 51.9 jit_solution(5115552057982432506)
XLA Ops:
  0.0 49.7 %cycle.1 = f32[32,32,128]{2,1,0:T(8,128)} custom-call(f32[1024,128]{1,0:T(8,128)} %bitcast.9, f32[1024,128]{1,0:T(8,128)} %bitcast.10, s32[32,128]{1,0:T(8,128)} %refs_0_.1, f32[32,128]{1,0:T(8,128)} %refs_1_.1, s32[2,32]{1,0:T(2,128)} %bitcast.13, f32[1,64]{1,0:T(1,128)} %bitcast.14, bf16[64,512]{1,0:T(8,128)(2,1)} %refs_4_.1, f32[1,512]{1,0:T(1,128)} %bitcast.12, ...), custom_call_target="tpu_custom_call" | custom-call | tf_op jit(solution)/shard_map/cycle/pallas_call | solution.py:409
  49.8 2.1 %copy.11 = f32[32,32,128]{2,1,0:T(8,128)} copy(f32[32,32,128]{2,0,1:T(8,128)} %bitcast.8) | data formatting | bytes 1048576 | tf_op jit(solution)/shard_map/transpose | solution.py:435

commit v3 on v2

--- a/solution.py
+++ b/solution.py
@@ -11,6 +11,10 @@
 F32 = jnp.float32
 BF16 = jnp.bfloat16
 MESH = pl.DeviceIdType.MESH
+PRIOR_TURNS = (0, 1)
+PERT_TURNS = (0, 1)
+TURN_AT = {1: 1, 3: 2, 6: 4}
+OUT_TURNS = (2, 1)
 
 
 def dot1(a, b):
@@ -51,7 +55,7 @@
         p = step(jnp.where(la | lb, 0.0, p), a, b)
     return p
 
-def inverses(mats, nb=16):
+def inverses(mats, nb=16, between=None):
     size = mats[0].shape[0]
     rows = lax.broadcasted_iota(jnp.int32, (8, size), 0)
     lanes = lax.broadcasted_iota(jnp.int32, (8, size), 1)
@@ -86,6 +90,8 @@
                 t = a[lo + nb:]
                 out.append(jnp.where(hole[lo + nb:], 0.0, t) - doth(t, pad))
             mats[k] = jnp.concatenate(out, axis=0)
+        if between is not None:
+            between(lo // nb)
     return mats
 
 
@@ -130,9 +136,22 @@
     right = (holder(lax.rem(win + 1, n), rsp), rsp)
     left = (holder(lax.rem(win + n - 1, n), lsp), lsp)
 
-    def partner(i):
-        g = lax.rem(my_group + groups - i // gs, groups)
-        return g * gs + lax.rem(me + lax.rem(i, gs), gs)
+    def facing(t, turns):
+        k = lax.rem(turns[0] + groups + turns[1] * t, groups)
+        g, bit = 0, 1
+        while bit < groups:
+            g = g + lax.rem(my_group // bit + k // bit, 2) * bit
+            bit *= 2
+        return g
+
+    def each_peer(start, stop, turns, act):
+        @pl.loop(start * gs, stop * gs)
+        def _(i):
+            d = facing(i // gs, turns) * gs + lax.rem(me + lax.rem(i, gs), gs)
+
+            @pl.when(d != me)
+            def _():
+                act(d)
 
     loads = [pltpu.make_async_copy(prior_in, raw, loc.at[0]), pltpu.make_async_copy(pert_in, rawp, loc.at[1])]
     loads += [pltpu.make_async_copy(a, b, loc.at[3 + i]) for i, (a, b) in enumerate(zip(small_in, small))]
@@ -175,10 +194,10 @@
             src_ref=src.at[pl.ds(window(s, sp) * count, count)], dst_ref=dst.at[:, mine(s), :],
             send_sem=ss.at[s], recv_sem=rs.at[s], device_id=(s, sp), device_id_type=MESH)
 
-    @pl.loop(1, n)
-    def _(k):
-        fwd(prior, xb, xs, xr, partner(k)).start()
-
+    def send_pert(start, stop):
+        each_peer(start, stop, PERT_TURNS, lambda d: fwd(pert, pb, ps, pr, d).start())
+
+    each_peer(0, groups, PRIOR_TURNS, lambda d: fwd(prior, xb, xs, xr, d).start())
     keep(prior, xb)
     for load in loads[1:]:
         load.wait()
@@ -230,7 +249,7 @@
 
     @pl.loop(0, groups)
     def _(t):
-        g = lax.rem(my_group + t, groups)
+        g = facing(t, PRIOR_TURNS)
         for q in range(gs):
             s = g * gs + q
 
@@ -255,10 +274,7 @@
         halo(yb, rows, ys, yr, g, 0).start()
         halo(yb, rows, ys, yr, g, 1).start()
 
-    @pl.loop(1, n)
-    def _(k):
-        fwd(pert, pb, ps, pr, partner(k)).start()
-
+    send_pert(0, groups)
     w = width
     eye = jnp.where(ri == ci, 1.0, 0.0)
 
@@ -287,7 +303,13 @@
 
     last_one = count + 1
     for i in range(1, count + 1):
-        multiply(i, [j for j in range(i, min(i + 2, count) + 1)], [c for c in range(count) if abs(c + 1 - i) < 2])
+        multiply(i, range(max(1, i - 2), min(i + 2, count) + 1), [c for c in range(count) if abs(c + 1 - i) < 2])
+
+    pinv = inverses([yy[i, i] + eye for i in range(1, count + 1)])
+    both = [on_left[c] * on_right[c] for c in range(count)]
+    swap = [c + 2 if c + 1 < count else c for c in range(count)]
+    ps1 = [either(both[c], pinv[swap[c] - 1], pinv[c]) for c in range(count)]
+    fs = [doth(ps1[c], either(both[c], yx[swap[c], c], yx[c + 1, c])) for c in range(count)]
 
     @pl.loop(0, groups)
     def _(g):
@@ -296,25 +318,33 @@
 
     obs[0] = anomaly(yb[0])
     obs[last_one] = anomaly(yb[last_one])
-    multiply(0, [j for j in range(0, min(2, last_one) + 1)], [0])
-    for i in range(max(1, last_one - 2), last_one):
-        multiply(i, [last_one], [])
-    multiply(last_one, [last_one], [count - 1])
-
-    s11, s12, s22, g1, g2 = [], [], [], [], []
+    multiply(0, [0, 1, 2], [0])
+    multiply(last_one, [last_one, last_one - 1, last_one - 2], [count - 1])
+
+    def second(c, left_one, right_one):
+        if c + 1 < count:
+            return either(on_left[c], left_one, right_one)
+        return either(on_right[c], right_one, left_one)
+
+    ets, ts, gs2 = [], [], []
     for c in range(count):
         e = c + 1
-        s11.append(either(on_left[c], yy[e - 1, e - 1], yy[e, e]) + eye)
-        s22.append(either(on_right[c], yy[e + 1, e + 1], yy[e, e]) + eye)
-        s12.append(either(on_left[c], either(on_right[c], yy[e - 1, e + 1], yy[e - 1, e]), yy[e, e + 1]))
-        g1.append(either(on_left[c], yx[e - 1, c], yx[e, c]))
-        g2.append(either(on_right[c], yx[e + 1, c], yx[e, c]))
-    s21 = [m.T for m in s12]
+        far = swap[c]
+        near_l, near_r = yy[e - 1, e], yy[e + 1, e]
+        if far > e:
+            s21 = second(c, either(both[c], yy[e - 1, far], near_l), near_r)
+        else:
+            s21 = second(c, near_l, either(both[c], yy[e + 1, far], near_r))
+        et = doth(s21, ps1[c])
+        ets.append(et)
+        ts.append(second(c, yy[e - 1, e - 1], yy[e + 1, e + 1]) + eye - lax.dot_general(
+            et, s21, (((1,), (1,)), ((), ())), preferred_element_type=F32, precision=lax.Precision.HIGHEST))
+        gs2.append(second(c, yx[e - 1, c], yx[e + 1, c]) - doth(s21, fs[c]))
 
     def innovate(start, stop):
         @pl.loop(start, stop)
         def _(t):
-            g = lax.rem(my_group + t, groups)
+            g = facing(t, PERT_TURNS)
             for q in range(gs):
                 s = g * gs + q
 
@@ -328,18 +358,19 @@
             halo(ib, rows, isd, ir, g, 0).start()
             halo(ib, rows, isd, ir, g, 1).start()
 
-    pinv = inverses(s11)
-    innovate(0, 2)
-    es = [doth(pinv[c], s12[c]) for c in range(count)]
-    ts = [s22[c] - doth(s21[c], es[c]) for c in range(count)]
-    fs = [doth(pinv[c], g1[c]) for c in range(count)]
-    tinv = inverses(ts)
-    innovate(2, groups)
-    gains = []
-    for c in range(count):
-        k2 = doth(tinv[c], g2[c] - doth(s21[c], fs[c]))
-        k1 = fs[c] - doth(es[c], k2)
-        gains.append(jnp.concatenate([k1, k2], axis=0))
+    done = [0]
+
+    def innovate_to(quarters):
+        stop = groups * quarters // 4
+        if stop > done[0]:
+            innovate(done[0], stop)
+            done[0] = stop
+
+    innovate_to(0)
+    tinv = inverses(ts, between=lambda k: innovate_to(TURN_AT.get(k, 0)))
+    ks = [doth(tinv[c], gs2[c]) for c in range(count)]
+    gains = [jnp.concatenate([fs[c] - doth(ets[c].T, ks[c]), ks[c]], axis=0) for c in range(count)]
+    innovate_to(4)
 
     def back(d):
         return pltpu.make_async_remote_copy(
@@ -354,25 +385,19 @@
     gh = [split(m) for m in gains]
 
     def pick(c, rows):
-        mid = ib[c + 1, rows, :]
-        return jnp.concatenate(
-            [either(on_left[c], ib[c, rows, :], mid), either(on_right[c], ib[c + 2, rows, :], mid)], axis=1)
+        near_one = either(both[c], ib[swap[c], rows, :], ib[c + 1, rows, :])
+        return jnp.concatenate([near_one, second(c, ib[c, rows, :], ib[c + 2, rows, :])], axis=1)
 
     @pl.loop(0, groups)
     def _(t):
-        g = lax.rem(my_group + groups // 2 + t, groups)
+        g = facing(t, OUT_TURNS)
         rows = group_rows(g)
         for side in range(2):
             halo(ib, rows, isd, ir, g, side).wait_recv()
         for c in range(count):
             ih, il = split(pick(c, rows))
             res[c, rows, :] = xb[c, rows, :] + dot1(ih, gh[c][0]) + dot1(ih, gh[c][1]) + dot1(il, gh[c][0])
-        for q in range(gs):
-            d = g * gs + lax.rem(me + q, gs)
-
-            @pl.when(d != me)
-            def _():
-                back(d).start()
+        each_peer(t, t + 1, OUT_TURNS, lambda d: back(d).start())
 
     last = pltpu.make_async_copy(res.at[:, mine(me), :], out.at[pl.ds(first, count)], loc.at[2])
     last.start()
@@ -429,9 +454,10 @@
             dma((n,)), dma((n,)), dma((3 + len(small),)),
         ],
         compiler_params=pltpu.CompilerParams(
-            collective_id=0, has_side_effects=True, vmem_limit_bytes=67043328),
+            collective_id=0, has_side_effects=True, vmem_limit_bytes=50331648),
         name="cycle",
-    )(prior.reshape(each * span, width), pert.reshape(each * span, width), *small)
+    )(*[pltpu.with_memory_space_constraint(v, pltpu.HBM) for v in (
+        prior.reshape(each * span, width), pert.reshape(each * span, width), *small)])
     return jnp.transpose(out, (1, 0, 2))
 
 

time: 52.9 us -> 50.3 us (0.951)
  local copies, waits for them, and re-layouts: 2.14 us -> 1.1 us
  Pallas kernels: 49.7 us -> 48.7 us
    transpose x1, local copies, waits for them, and re-layouts: 2.14 us -> 1.1 us  [body(): return jnp.transpose(out, (1, 0, 2))]
    pallas_call x1, Pallas kernels: 49.7 us -> 48.7 us  [body(): pl.pallas_call(functools.partial(kernel, n, ns), out_shape=jax.ShapeDtype...]
where the time goes in v3:
time: 50.3 us; the launch traced here: 49.8 us
  Pallas kernels  48.7 us (97%)
  local copies, waits for them, and re-layouts  1.1 us (2%)
    pallas_call x1, Pallas kernels, body(): pl.pallas_call(functools.partial(kernel, n, ns), out_shape=jax.ShapeDtype...  48.7 us
    transpose x1, local copies, waits for them, and re-layouts, body(): return jnp.transpose(out, (1, 0, 2))  1.1 us

profile of v3, /device:TPU:9, one launch (start us, length us, event | category | flops | bytes accessed | tf_op | source)
XLA Modules:
  0.0 49.8 jit_solution(17695896368860087134)
XLA Ops:
  0.0 48.7 %cycle.1 = f32[32,32,128]{2,1,0:T(8,128)S(1)} custom-call(f32[1024,128]{1,0:T(8,128)} %bitcast.9, f32[1024,128]{1,0:T(8,128)} %bitcast.10, s32[32,128]{1,0:T(8,128)} %refs_0_.1, f32[32,128]{1,0:T(8,128)} %refs_1_.1, s32[2,32]{1,0:T(2,128)} %bitcast.13, f32[1,64]{1,0:T(1,128)} %bitcast.14, bf16[64,512]{1,0:T(8,128)(2,1)} %refs_4_.1, f32[1,512]{1,0:T(1,128)} %bitcast.12, ...), custom_call_target="tpu_custom_call" | custom-call | tf_op jit(solution)/shard_map/cycle/pallas_call | solution.py:434
  48.7 1.1 %copy.11 = f32[32,32,128]{2,1,0:T(8,128)} copy(f32[32,32,128]{2,0,1:T(8,128)S(1)} %bitcast.8) | data formatting | bytes 1048576 | tf_op jit(solution)/shard_map/transpose | solution.py:461

commit v4 on v3

--- a/solution.py
+++ b/solution.py
@@ -13,8 +13,8 @@
 MESH = pl.DeviceIdType.MESH
 PRIOR_TURNS = (0, 1)
 PERT_TURNS = (0, 1)
-TURN_AT = {1: 1, 3: 2, 6: 4}
-OUT_TURNS = (2, 1)
+TURN_AT = {0: 1, 2: 2, 6: 4}
+OUT_TURNS = (0, 1)
 
 
 def dot1(a, b):
@@ -195,7 +195,14 @@
             send_sem=ss.at[s], recv_sem=rs.at[s], device_id=(s, sp), device_id_type=MESH)
 
     def send_pert(start, stop):
-        each_peer(start, stop, PERT_TURNS, lambda d: fwd(pert, pb, ps, pr, d).start())
+        @pl.loop(0, n)
+        def _(i):
+            k = i // 2 // gs + lax.rem(i, 2) * (groups // 2)
+            d = facing(k, PERT_TURNS) * gs + lax.rem(me + lax.rem(i // 2, gs), gs)
+
+            @pl.when(d != me)
+            def _():
+                fwd(pert, pb, ps, pr, d).start()
 
     each_peer(0, groups, PRIOR_TURNS, lambda d: fwd(prior, xb, xs, xr, d).start())
     keep(prior, xb)
@@ -344,7 +351,7 @@
     def innovate(start, stop):
         @pl.loop(start, stop)
         def _(t):
-            g = facing(t, PERT_TURNS)
+            g = facing(t // 2 + lax.rem(t, 2) * (groups // 2), PERT_TURNS)
             for q in range(gs):
                 s = g * gs + q
 
@@ -390,14 +397,19 @@
 
     @pl.loop(0, groups)
     def _(t):
-        g = facing(t, OUT_TURNS)
+        g = facing(t // 2 + lax.rem(t + 1, 2) * (groups // 2), OUT_TURNS)
         rows = group_rows(g)
         for side in range(2):
             halo(ib, rows, isd, ir, g, side).wait_recv()
         for c in range(count):
             ih, il = split(pick(c, rows))
             res[c, rows, :] = xb[c, rows, :] + dot1(ih, gh[c][0]) + dot1(ih, gh[c][1]) + dot1(il, gh[c][0])
-        each_peer(t, t + 1, OUT_TURNS, lambda d: back(d).start())
+        for q in range(gs):
+            d = g * gs + lax.rem(me + q, gs)
+
+            @pl.when(d != me)
+            def _():
+                back(d).start()
 
     last = pltpu.make_async_copy(res.at[:, mine(me), :], out.at[pl.ds(first, count)], loc.at[2])
     last.start()

time: 50.3 us -> 49.8 us (0.990)
    pallas_call x1, Pallas kernels: 48.7 us -> 48.2 us  [body(): pl.pallas_call(functools.partial(kernel, n, ns), out_shape=jax.ShapeDtype...]
where the time goes in v4:
time: 49.8 us; the launch traced here: 49.3 us
  Pallas kernels  48.2 us (97%)
  local copies, waits for them, and re-layouts  1.1 us (2%)
    pallas_call x1, Pallas kernels, body(): pl.pallas_call(functools.partial(kernel, n, ns), out_shape=jax.ShapeDtype...  48.2 us
    transpose x1, local copies, waits for them, and re-layouts, body(): return jnp.transpose(out, (1, 0, 2))  1.1 us

profile of v4, /device:TPU:9, one launch (start us, length us, event | category | flops | bytes accessed | tf_op | source)
XLA Modules:
  0.0 49.3 jit_solution(5865420300600076705)
XLA Ops:
  0.0 48.2 %cycle.1 = f32[32,32,128]{2,1,0:T(8,128)S(1)} custom-call(f32[1024,128]{1,0:T(8,128)} %bitcast.9, f32[1024,128]{1,0:T(8,128)} %bitcast.10, s32[32,128]{1,0:T(8,128)} %refs_0_.1, f32[32,128]{1,0:T(8,128)} %refs_1_.1, s32[2,32]{1,0:T(2,128)} %bitcast.13, f32[1,64]{1,0:T(1,128)} %bitcast.14, bf16[64,512]{1,0:T(8,128)(2,1)} %refs_4_.1, f32[1,512]{1,0:T(1,128)} %bitcast.12, ...), custom_call_target="tpu_custom_call" | custom-call | tf_op jit(solution)/shard_map/cycle/pallas_call | solution.py:446
  48.2 1.1 %copy.11 = f32[32,32,128]{2,1,0:T(8,128)} copy(f32[32,32,128]{2,0,1:T(8,128)S(1)} %bitcast.8) | data formatting | bytes 1048576 | tf_op jit(solution)/shard_map/transpose | solution.py:473
